TPU v7x, 128 devices: a whole 4x4x4 slice. The times are simulated.
128 devices in a mesh: dp: 8 (over z, core), mp: 16 (over x, y).
Axes of the slice: x: 4, y: 4, z: 4, core: 2. Of those that a mesh axis runs over, the one named last changes fastest.
Arguments:
- features: bfloat16 [8192, 2048], P('dp'), may hold values from -21 to 21
- rewards: float32 [32, 256], P('dp'), may hold values from -6 to 6
- old_values: float32 [32, 256], P('dp'), may hold values from -6 to 6
- dones: int32 [32, 256], P('dp'), may hold values 0 or 1
- lengths: int32 [32], P('dp'), may hold values from 128 to 256
- proj_weights: bfloat16 [2048, 2, 8192], P(None, None, 'mp'), may hold values from -0.125 to 0.125
- down_weight: bfloat16 [8192, 2048], P('mp'), may hold values from -0.0625 to 0.0625
- value_head: float32 [2048], replicated, may hold values from -0.0078125 to 0.0078125
- master: float32 [2048, 2, 8192], P('dp', None, 'mp'), may hold values from -0.125 to 0.125
- moment: float32 [2048, 2, 8192], P('dp', None, 'mp'), may hold values from -1.035801e-05 to 1.035801e-05
- second: float32 [2048, 2, 8192], P('dp', None, 'mp'), may hold values from 2.9802322e-13 to 2.9802322e-12
Outputs:
- master_new: float32 [2048, 2, 8192], P('dp', None, 'mp')
- moment_new: float32 [2048, 2, 8192], P('dp', None, 'mp')
- second_new: float32 [2048, 2, 8192], P('dp', None, 'mp')
- working: bfloat16 [2048, 2, 8192], P(None, None, 'mp')
- total_loss: float32 [], replicated
All inputs are finite; a program needn't handle non-finite values. No bound on the sum of `dones` on one device may be relied on, other than what follows from the above.
Results may differ from a plain program's by a relative error of at most 0.0011.
Values may be sent and summed in bfloat16 or wider, within the bound.
A program may use at most 128 MiB of HBM per device.

v0:
```python
import functools
import math
import jax
import jax.numpy as jnp
from jax import lax
from jax.sharding import Mesh
from jax.sharding import PartitionSpec as P

DP = ("dp_0", "dp_1")
MP = ("mp_0", "mp_1")
DP_MP = ("dp_0", "dp_1", "mp_0", "mp_1")
GAMMA = 0.99
LAMBDA = 0.95
MAX_NORM = 0.05


def own_block(parts, axes, sequence):
    shape = [lax.axis_size(a) for a in axes]
    parts = parts.reshape(*shape, *parts.shape[1:])
    parts = parts.transpose(*sequence, *range(len(axes), parts.ndim))
    parts = parts.reshape(-1, *parts.shape[len(axes) :])
    for k in sequence:
        parts = lax.psum_scatter(parts, axes[k], scatter_dimension=0, tiled=True)
    return parts[0]


def in_blocks(value, dim, count):
    before, after = (value.shape[:dim], value.shape[dim + 1 :])
    return jnp.moveaxis(value.reshape(*before, count, -1, *after), dim, 0)


def summed_rows(value, axes, sequence, dim):
    count = lax.axis_size(axes)
    return own_block(in_blocks(value, dim, count), axes, sequence)


def one_axis_at_a_time(value, axes):
    return functools.reduce(lax.psum, axes, value)


def gae_targets(rewards, old_values, dones, lengths):
    seq_len = rewards.shape[1]
    keeps = 1.0 - dones.astype(jnp.float32)
    following = jnp.concatenate([old_values[:, 1:], jnp.zeros_like(old_values[:, :1])], axis=1)
    deltas = rewards + GAMMA * following * keeps - old_values
    counted = jnp.cumsum(dones, axis=1) - dones
    places = jnp.arange(seq_len, dtype=jnp.int32)
    spans = places[None, :] - places[:, None]
    linked = (counted[:, :, None] == counted[:, None, :]) & (spans[None] >= 0)
    powers = jnp.exp(jnp.maximum(spans, 0).astype(jnp.float32) * math.log(GAMMA * LAMBDA))
    kernel = jnp.where(linked, powers[None], jnp.zeros((), jnp.float32))
    advantage = jnp.einsum("ats,as->at", kernel, deltas, precision=lax.Precision.HIGHEST)
    targets = (advantage + old_values).reshape(-1)
    mask = (places[None, :] < lengths[:, None]).astype(jnp.float32).reshape(-1)
    return (targets, mask)


def value_loss(features, mixed, targets, mask, value_head, total_tokens):
    stream = features.astype(jnp.float32) + mixed
    norm_factor = lax.rsqrt(jnp.mean(stream * stream, axis=-1) + 1e-05)
    normed = stream * norm_factor[:, None]
    estimate = jnp.dot(normed, value_head, precision=lax.Precision.HIGHEST)
    errors = estimate - targets
    loss_part = jnp.sum(mask * errors * errors) / total_tokens
    coeff = 2.0 * mask * errors / total_tokens
    head_grad = coeff[:, None] * value_head[None, :]
    out_grad = (
        norm_factor[:, None]
        * (head_grad - normed * jnp.mean(head_grad * normed, axis=-1, keepdims=True))
    ).astype(jnp.bfloat16)
    return (loss_part, out_grad)


def contract_rows(left, right):
    return lax.dot_general(
        left, right, (((0,), (0,)), ((), ())), preferred_element_type=jnp.float32
    )


def per_device(
    features,
    rewards,
    old_values,
    dones,
    lengths,
    proj_weights,
    down_weight,
    value_head,
    master,
    moment,
    second,
):
    token_count = features.shape[0]
    model_width = features.shape[1]
    ff_local = down_weight.shape[0]
    data_ways = lax.axis_size(DP)
    model_ways = lax.axis_size(MP)
    total_tokens = token_count * data_ways
    targets, mask = gae_targets(rewards, old_values, dones, lengths)
    both = jnp.dot(
        features,
        proj_weights.reshape(model_width, 2 * ff_local),
        preferred_element_type=jnp.float32,
    )
    both = both.reshape(token_count, 2, ff_local)
    gate_values = both[:, 0, :]
    up_values = both[:, 1, :]
    hidden = (jax.nn.silu(gate_values) * up_values).astype(jnp.bfloat16)
    mixed = lax.psum(
        jnp.dot(hidden, down_weight, preferred_element_type=jnp.float32).astype(jnp.bfloat16), MP
    ).astype(jnp.float32)
    loss_part, out_grad = value_loss(features, mixed, targets, mask, value_head, total_tokens)
    loss_part = loss_part / model_ways
    hidden_grad = jnp.dot(out_grad, down_weight.T, preferred_element_type=jnp.float32)
    gate_sigmoid = jax.nn.sigmoid(gate_values)
    gate_grad = (
        hidden_grad * up_values * gate_sigmoid * (1.0 + gate_values * (1.0 - gate_sigmoid))
    ).astype(jnp.bfloat16)
    up_grad = (hidden_grad * gate_values * gate_sigmoid).astype(jnp.bfloat16)
    both_grad = jnp.stack([gate_grad, up_grad], axis=1).reshape(token_count, 2 * ff_local)
    row_share = model_width // data_ways
    grads = summed_rows(
        contract_rows(features, both_grad).reshape(row_share * lax.axis_size(DP), 2, ff_local),
        DP,
        (1, 0),
        0,
    )
    squares = jnp.sum(grads * grads)
    squared_total, total_loss = (
        one_axis_at_a_time(squares, DP_MP),
        one_axis_at_a_time(loss_part, DP_MP),
    )
    clip = jnp.minimum(1.0, MAX_NORM / (jnp.sqrt(squared_total) + 1e-06))
    clipped = clip * grads
    moment_new = 0.9 * moment + 0.1 * clipped
    second_new = 0.999 * second + 0.001 * clipped * clipped
    first_hat = moment_new / (1.0 - 0.9**10)
    second_hat = second_new / (1.0 - 0.999**10)
    master_new = master - 0.001 * (first_hat / (jnp.sqrt(second_hat) + 1e-08) + 0.1 * master)
    working = lax.all_gather(master_new.astype(jnp.bfloat16), DP, axis=0, tiled=True)
    return (master_new, moment_new, second_new, working, total_loss)


def solution(mesh):
    finer = Mesh(mesh.devices.reshape(4, 2, 4, 4), ("dp_0", "dp_1", "mp_0", "mp_1"))
    return jax.shard_map(
        per_device,
        mesh=finer,
        in_specs=(
            P(DP, None),
            P(DP, None),
            P(DP, None),
            P(DP, None),
            P(DP),
            P(None, None, MP),
            P(MP, None),
            P(),
            P(DP, None, MP),
            P(DP, None, MP),
            P(DP, None, MP),
        ),
        out_specs=(P(DP, None, MP), P(DP, None, MP), P(DP, None, MP), P(None, None, MP), P()),
        check_vma=False,
    )
```

profile of v0, /device:TPU:1, one launch (start us, length us, event | category | flops | bytes accessed | tf_op | source)
XLA Modules:
  0.0 348.5 jit_solution(17223176488133655442)
XLA Ops:
  7.2 5.5 %copy.34 = bf16[256,8,2,512]{3,1,2,0:T(8,128)(2,1)} copy(bf16[256,8,2,512]{3,2,1,0:T(2,128)(2,1)} %bitcast.73) | data formatting | bytes 8388608
  12.8 6.5 %copy.21 = bf16[1024,2048]{1,0:T(8,128)(2,1)} copy(bf16[1024,2048]{0,1:T(8,128)(2,1)} %bitcast.72) | data formatting | bytes 8388608 | tf_op jit(solution)/shard_map/dot_general | solution.py:100
  19.3 7.6 %fusion.6 = f32[1024,2,512]{0,2,1:T(8,128)S(1)} fusion(bf16[2,512,2048]{2,1,0:T(8,128)(2,1)} %bitcast.74, bf16[1024,2048]{1,0:T(8,128)(2,1)} %param.11), kind=kOutput, calls=%fused_computation.10 | convolution fusion | flops 4294967296 | bytes 12582912 | tf_op jit(solution)/shard_map/dot_general | solution.py:100
  26.9 2.0 copy-done.9
  28.9 4.4 %convolution_convert_fusion = bf16[1024,2048]{1,0:T(8,128)(2,1)} fusion(bf16[512,2048]{1,0:T(8,128)(2,1)S(1)} %copy-done, f32[1024,2,512]{0,2,1:T(8,128)S(1)} %fusion.6), kind=kOutput, calls=%fused_computation.14 | convolution fusion | flops 2152726528 | bytes 10485760 | tf_op jit(solution)/shard_map/dot_general | solution.py:110
  37.1 102.5 %all-reduce.7.cloned.1.call-done = bf16[1024,2048]{1,0:T(8,128)(2,1)} async-done(((bf16[1024,2048]{1,0:T(8,128)(2,1)}), bf16[1024,2048]{1,0:T(8,128)(2,1)}) %all-reduce.7.cloned.1.call-update) | async-done | bytes 4194320 | tf_op jit(solution)/shard_map/psum | solution.py:109
  139.7 5.0 %multiply_reduce_fusion = f32[1024]{0:T(1024)S(1)} fusion(bf16[1024,2048]{1,0:T(8,128)(2,1)} %all-reduce.7.cloned.1.call-done, bf16[1024,2048]{1,0:T(8,128)(2,1)} %param.11), kind=kLoop, calls=%fused_computation.5 | loop fusion | flops 10484736 | bytes 8392704 | tf_op jit(solution)/shard_map/reduce_sum | solution.py:60
  145.6 8.1 %fusion.4 = f32[1,1024]{1,0:T(1,128)S(1)} fusion(f32[2048,1]{0,1:T(1,128)S(1)} %bitcast.76, bf16[1024,2048]{1,0:T(8,128)(2,1)S(1)} %copy-done.3, bf16[1024,2048]{1,0:T(8,128)(2,1)S(1)} %copy-done.2, f32[1024]{0:T(1024)S(1)} %add_rsqrt_fusion), kind=kOutput, calls=%fused_computation.8 | convolution fusion | flops 33554432 | bytes 8404992 | tf_op jit(solution)/shard_map/dot_general | solution.py:62
  154.4 2.6 fusion
  156.9 5.4 %fusion.19 = (bf16[1024,1,512]{0,2,1:T(8,128)(2,1)S(1)}, bf16[1024,1,512]{0,2,1:T(8,128)(2,1)S(1)}) fusion(f32[1024,2,512]{0,2,1:T(8,128)S(1)} %copy-done.10, bf16[512,2048]{1,0:T(8,128)(2,1)S(1)} %copy-done, bf16[1024,2048]{1,0:T(8,128)(2,1)S(1)} %copy-done.3, bf16[1024,2048]{1,0:T(8,128)(2,1)S(1)} %copy-done.2, f32[1024]{0:T(1024)S(1)} %broadcast_multiply_fusion, ...), kind=kOutput, calls=%fused_computation.36 | convolution fusion | flops 2173173760 | bytes 16797696 | tf_op jit(solution)/shard_map/dot_general | solution.py:114
  162.6 6.7 %convolution_bitcast_fusion = f32[2048,1024]{0,1:T(8,128)} fusion(bf16[1024,1024]{0,1:T(8,128)(2,1)S(1)} %bitcast.75, bf16[1024,2048]{1,0:T(8,128)(2,1)S(1)} %copy-done.2), kind=kOutput, calls=%fused_computation.9 | convolution fusion | flops 4294967296 | bytes 14680064 | tf_op jit(solution)/shard_map/dot_general | solution.py:75
  169.3 11.7 %reshape_reshape_reshape.3 = f32[4,2,256,2,512]{2,1,0,4,3:T(2,128)} reshape(f32[2048,1024]{0,1:T(8,128)} %convolution_bitcast_fusion) | data formatting | bytes 16777216 | tf_op jit(solution)/shard_map/reshape;reshape;reshape | solution.py:19
  181.0 13.1 %copy.24 = f32[2,4,256,2,512]{4,2,3,1,0:T(8,128)} copy(f32[2,4,256,2,512]{2,0,1,4,3:T(2,128)} %bitcast.71) | data formatting | bytes 16777216 | tf_op jit(solution)/shard_map/transpose | solution.py:20
  194.2 19.7 %reduce-scatter.3.cloned.1.call-done = f32[4,256,2,512]{3,1,2,0:T(8,128)} async-done(((f32[8,256,2,512]{3,1,2,0:T(8,128)}), f32[4,256,2,512]{3,1,2,0:T(8,128)}) %reduce-scatter.3.cloned.1.call-update) | async-done | bytes 4194320 | tf_op jit(solution)/shard_map/reduce_scatter | solution.py:23
  214.6 49.8 %reduce-scatter.5.cloned.1.call-done = f32[1,256,2,512]{3,1,2,0:T(8,128)} async-done(((f32[4,256,2,512]{3,1,2,0:T(8,128)}), f32[1,256,2,512]{3,1,2,0:T(8,128)}) %reduce-scatter.5.cloned.1.call-update) | async-done | bytes 1048592 | tf_op jit(solution)/shard_map/reduce_scatter | solution.py:23
  264.4 2.1 multiply_reduce_fusion.1
  266.5 7.1 %all-reduce.3 = (f32[]{:T(128)}, f32[]{:T(128)}) all-reduce(f32[]{:T(128)} %multiply_reduce_fusion.1, f32[]{:T(128)S(6)} %div.55), channel_id=1, replica_groups=mesh['dp_0'=4,'dp_1'=2,'mp_0'=4,'mp_1'=4] {'dp_0'}, use_global_device_ids=true, to_apply=%region_8.9 | all-reduce | flops 2 | bytes 16 | tf_op jit(solution)/shard_map/psum | solution.py:38
  273.6 5.5 %all-reduce.4 = (f32[]{:T(128)}, f32[]{:T(128)}) all-reduce(f32[]{:T(128)} %get-tuple-element.14, f32[]{:T(128)} %get-tuple-element.15), channel_id=1, replica_groups=mesh['dp_0'=4,'dp_1'=2,'mp_0'=4,'mp_1'=4] {'dp_1'}, use_global_device_ids=true, to_apply=%region_9.10 | all-reduce | flops 2 | bytes 16 | tf_op jit(solution)/shard_map/psum | solution.py:38
  279.1 9.0 %all-reduce.2 = (f32[]{:T(128)}, f32[]{:T(128)}) all-reduce(f32[]{:T(128)} %get-tuple-element.16, f32[]{:T(128)} %get-tuple-element.17), channel_id=1, replica_groups=mesh['dp_0'=4,'dp_1'=2,'mp_0'=4,'mp_1'=4] {'mp_0'}, use_global_device_ids=true, to_apply=%region_10.11 | all-reduce | flops 2 | bytes 16 | tf_op jit(solution)/shard_map/psum | solution.py:38
  288.1 9.1 %all-reduce.1 = (f32[]{:T(128)}, f32[]{:T(128)}) all-reduce(f32[]{:T(128)} %get-tuple-element.12, f32[]{:T(128)} %get-tuple-element.13), channel_id=1, replica_groups=mesh['dp_0'=4,'dp_1'=2,'mp_0'=4,'mp_1'=4] {'mp_1'}, use_global_device_ids=true, to_apply=%region_11.12 | all-reduce | flops 2 | bytes 16 | tf_op jit(solution)/shard_map/psum | solution.py:38
  297.9 3.2 fusion.31
  302.5 1.8 copy.29
  307.8 26.3 %all-gather.2.cloned.1.call-done = bf16[2048,2,512]{2,1,0:T(2,128)(2,1)} async-done(((bf16[256,2,512]{2,1,0:T(2,128)(2,1)}), bf16[2048,2,512]{2,1,0:T(2,128)(2,1)}) %all-gather.2.cloned.1.call-update) | async-done | bytes 4194320 | tf_op jit(solution)/shard_map/all_gather | solution.py:140
  334.1 7.8 %copy.53 = bf16[2048,2,512]{2,1,0:T(2,128)(2,1)} copy(bf16[2048,2,512]{2,1,0:T(2,128)(2,1)} %all-gather.2.cloned.1.call-done) | data formatting | bytes 8388608
  (54 shorter events, 10.5 us)
Async XLA Ops:
  7.2 21.7 %copy-start = (bf16[512,2048]{1,0:T(8,128)(2,1)S(1)}, bf16[512,2048]{1,0:T(8,128)(2,1)}, u32[]{:S(2)}) copy-start(bf16[512,2048]{1,0:T(8,128)(2,1)} %param.17) | copy-start | bytes 6291460
  7.2 132.5 %all-reduce.7.cloned.1.call-start = ((), (), s32[]{:S(2)}) async-start(), calls=%async_computation.2 | async-start | bytes 8388608 | tf_op jit(solution)/shard_map/psum | solution.py:109
  26.9 2.0 copy-start.9
  33.3 0.7 copy-start.8
  33.3 0.7 copy-start.5
  33.3 0.8 copy-start.4
  33.3 2.5 copy-start.7
  33.4 180.5 %reduce-scatter.3.cloned.1.call-start = ((), (), s32[]{:S(2)}) async-start(), calls=%async_computation.3 | async-start | bytes 12582912 | tf_op jit(solution)/shard_map/reduce_scatter | solution.py:23
  37.1 107.6 %copy-start.6 = (f32[2048]{0:T(1024)S(1)}, f32[2048]{0:T(1024)}, u32[]{:S(2)}) copy-start(f32[2048]{0:T(1024)} %param.18) | copy-start | bytes 24580
  139.7 5.1 %copy-start.2 = (bf16[1024,2048]{1,0:T(8,128)(2,1)S(1)}, bf16[1024,2048]{1,0:T(8,128)(2,1)}, u32[]{:S(2)}) copy-start(bf16[1024,2048]{1,0:T(8,128)(2,1)} %param.11) | copy-start | bytes 12582916
  139.7 5.9 %copy-start.3 = (bf16[1024,2048]{1,0:T(8,128)(2,1)S(1)}, bf16[1024,2048]{1,0:T(8,128)(2,1)}, u32[]{:S(2)}) copy-start(bf16[1024,2048]{1,0:T(8,128)(2,1)} %all-reduce.7.cloned.1.call-done) | copy-start | bytes 12582916
  154.3 2.6 copy-start.10
  194.1 70.3 %reduce-scatter.5.cloned.1.call-start = ((), (), s32[]{:S(2)}) async-start(), calls=%async_computation.4 | async-start | bytes 5242880 | tf_op jit(solution)/shard_map/reduce_scatter | solution.py:23
  213.9 120.2 %all-gather.2.cloned.1.call-start = ((), (), s32[]{:S(2)}) async-start(), calls=%async_computation.5 | async-start | bytes 4718592 | tf_op jit(solution)/shard_map/all_gather | solution.py:140
  334.1 7.9 %copy-start.1 = (bf16[512,2048]{1,0:T(8,128)(2,1)S(1)}, bf16[512,2048]{1,0:T(8,128)(2,1)}, u32[]{:S(2)}) copy-start(bf16[512,2048]{1,0:T(8,128)(2,1)} %param.17) | copy-start | bytes 6291460
Sparse Core Ops, SparseCore 0:
  33.5 106.1 all-reduce.6
  194.2 19.5 reduce-scatter.2
  216.3 48.0 reduce-scatter.4
  302.6 31.4 all-gather.1
where the time goes:
time: 350 us; the launch traced here: 348 us
  waiting for transfers between devices  198 us (57%)
  local copies, waits for them, and re-layouts  55.1 us (16%)
  matrix products  33.5 us (10%)
  blocking collectives  30.7 us (9%)
  other arithmetic  15.3 us (4%)
  between operations  15.3 us (4%)
    psum x1, waiting for transfers between devices, per_device(): lax.psum(jnp.dot(hidden, down_weight, preferred_element_type=jnp.float32)...  103 us
    reduce_scatter x2, waiting for transfers between devices, own_block(): parts = lax.psum_scatter(parts, axes[k], scatter_dimension=0, tiled=True)  69.5 us
    psum x4, blocking collectives, one_axis_at_a_time(): return functools.reduce(lax.psum, axes, value)  30.7 us
    all_gather x1, waiting for transfers between devices, per_device(): lax.all_gather(master_new.astype(jnp.bfloat16), DP, axis=0, tiled=True)  26.3 us
    unnamed x28, local copies, waits for them, and re-layouts  22 us
    transpose x1, local copies, waits for them, and re-layouts, own_block(): parts = parts.transpose(*sequence, *range(len(axes), parts.ndim))  13.1 us
    another operation x1, local copies, waits for them, and re-layouts, own_block(): parts = parts.reshape(*shape, *parts.shape[1:])  11.7 us
    dot_general x1, matrix products, value_loss(): estimate = jnp.dot(normed, value_head, precision=lax.Precision.HIGHEST)  8.13 us
  transfers between devices with their start and end apart: 4, of which 4 were waited for; matrix products, arithmetic and copies ran while one was open for 2% of the time, Pallas kernels for 0%

commit v1 on v0

--- a/solution.py
+++ b/solution.py
@@ -107,7 +107,11 @@
     up_values = both[:, 1, :]
     hidden = (jax.nn.silu(gate_values) * up_values).astype(jnp.bfloat16)
     mixed = lax.psum(
-        jnp.dot(hidden, down_weight, preferred_element_type=jnp.float32).astype(jnp.bfloat16), MP
+        lax.psum(
+            jnp.dot(hidden, down_weight, preferred_element_type=jnp.float32).astype(jnp.bfloat16),
+            "mp_1",
+        ),
+        "mp_0",
     ).astype(jnp.float32)
     loss_part, out_grad = value_loss(features, mixed, targets, mask, value_head, total_tokens)
     loss_part = loss_part / model_ways

time: 350 us -> 434 us (1.24)
  waiting for transfers between devices: 198 us -> 283 us
    psum x0 -> x1, waiting for transfers between devices: none -> 91.5 us  [per_device(): lax.psum(lax.psum(jnp.dot(hidden, down_weight, preferred_element_type=jnp...]
    psum x1, waiting for transfers between devices: 103 us -> 95.9 us  [per_device(): lax.psum(jnp.dot(hidden, down_weight, preferred_element_type=jnp.float32)...]
  transfers between devices with their start and end apart: 4 -> 5, of which waited for: 4 -> 5; matrix products, arithmetic and copies ran while one was open for 2% -> 2% of each run, Pallas kernels for 0% -> 0%
where the time goes in v1:
time: 434 us; the launch traced here: 433 us
  waiting for transfers between devices  283 us (65%)
  local copies, waits for them, and re-layouts  54.7 us (13%)
  matrix products  33.5 us (8%)
  blocking collectives  30.7 us (7%)
  other arithmetic  15.3 us (4%)
  between operations  15.3 us (4%)
    psum x1, waiting for transfers between devices, per_device(): lax.psum(jnp.dot(hidden, down_weight, preferred_element_type=jnp.float32)...  95.9 us
    psum x1, waiting for transfers between devices, per_device(): lax.psum(lax.psum(jnp.dot(hidden, down_weight, preferred_element_type=jnp...  91.5 us
    reduce_scatter x2, waiting for transfers between devices, own_block(): parts = lax.psum_scatter(parts, axes[k], scatter_dimension=0, tiled=True)  69.3 us
    psum x4, blocking collectives, one_axis_at_a_time(): return functools.reduce(lax.psum, axes, value)  30.7 us
    all_gather x1, waiting for transfers between devices, per_device(): lax.all_gather(master_new.astype(jnp.bfloat16), DP, axis=0, tiled=True)  26.3 us
    unnamed x28, local copies, waits for them, and re-layouts  21.6 us
    transpose x1, local copies, waits for them, and re-layouts, own_block(): parts = parts.transpose(*sequence, *range(len(axes), parts.ndim))  13.1 us
    another operation x1, local copies, waits for them, and re-layouts, own_block(): parts = parts.reshape(*shape, *parts.shape[1:])  11.7 us
  transfers between devices with their start and end apart: 5, of which 5 were waited for; matrix products, arithmetic and copies ran while one was open for 2% of the time, Pallas kernels for 0%

profile of v1, /device:TPU:1, one launch (start us, length us, event | category | flops | bytes accessed | tf_op | source)
XLA Modules:
  0.0 432.8 jit_solution(13909013748216045495)
XLA Ops:
  7.2 5.5 %copy.34 = bf16[256,8,2,512]{3,1,2,0:T(8,128)(2,1)} copy(bf16[256,8,2,512]{3,2,1,0:T(2,128)(2,1)} %bitcast.73) | data formatting | bytes 8388608
  12.8 6.5 %copy.21 = bf16[1024,2048]{1,0:T(8,128)(2,1)} copy(bf16[1024,2048]{0,1:T(8,128)(2,1)} %bitcast.72) | data formatting | bytes 8388608 | tf_op jit(solution)/shard_map/dot_general | solution.py:100
  19.3 7.6 %fusion.6 = f32[1024,2,512]{0,2,1:T(8,128)S(1)} fusion(bf16[2,512,2048]{2,1,0:T(8,128)(2,1)} %bitcast.74, bf16[1024,2048]{1,0:T(8,128)(2,1)} %param.11), kind=kOutput, calls=%fused_computation.10 | convolution fusion | flops 4294967296 | bytes 12582912 | tf_op jit(solution)/shard_map/dot_general | solution.py:100
  26.9 2.0 copy-done.9
  28.9 4.4 %convolution_convert_fusion = bf16[1024,2048]{1,0:T(8,128)(2,1)} fusion(bf16[512,2048]{1,0:T(8,128)(2,1)S(1)} %copy-done, f32[1024,2,512]{0,2,1:T(8,128)S(1)} %fusion.6), kind=kOutput, calls=%fused_computation.14 | convolution fusion | flops 2152726528 | bytes 10485760 | tf_op jit(solution)/shard_map/dot_general | solution.py:111
  33.4 95.9 %all-reduce.8.cloned.1.call-done = bf16[1024,2048]{1,0:T(8,128)(2,1)} async-done(((bf16[1024,2048]{1,0:T(8,128)(2,1)}), bf16[1024,2048]{1,0:T(8,128)(2,1)}) %all-reduce.8.cloned.1.call-update) | async-done | bytes 4194320 | tf_op jit(solution)/shard_map/psum | solution.py:110
  132.7 91.5 %all-reduce.10.cloned.1.call-done = bf16[1024,2048]{1,0:T(8,128)(2,1)} async-done(((bf16[1024,2048]{1,0:T(8,128)(2,1)}), bf16[1024,2048]{1,0:T(8,128)(2,1)}) %all-reduce.10.cloned.1.call-update) | async-done | bytes 4194320 | tf_op jit(solution)/shard_map/psum | solution.py:109
  224.3 5.0 %multiply_reduce_fusion = f32[1024]{0:T(1024)S(1)} fusion(bf16[1024,2048]{1,0:T(8,128)(2,1)} %all-reduce.10.cloned.1.call-done, bf16[1024,2048]{1,0:T(8,128)(2,1)} %param.11), kind=kLoop, calls=%fused_computation.5 | loop fusion | flops 10484736 | bytes 8392704 | tf_op jit(solution)/shard_map/reduce_sum | solution.py:60
  230.2 8.1 %fusion.4 = f32[1,1024]{1,0:T(1,128)S(1)} fusion(f32[2048,1]{0,1:T(1,128)S(1)} %bitcast.76, bf16[1024,2048]{1,0:T(8,128)(2,1)S(1)} %copy-done.3, bf16[1024,2048]{1,0:T(8,128)(2,1)S(1)} %copy-done.2, f32[1024]{0:T(1024)S(1)} %add_rsqrt_fusion), kind=kOutput, calls=%fused_computation.8 | convolution fusion | flops 33554432 | bytes 8404992 | tf_op jit(solution)/shard_map/dot_general | solution.py:62
  238.9 2.6 fusion
  241.5 5.4 %fusion.19 = (bf16[1024,1,512]{0,2,1:T(8,128)(2,1)S(1)}, bf16[1024,1,512]{0,2,1:T(8,128)(2,1)S(1)}) fusion(f32[1024,2,512]{0,2,1:T(8,128)S(1)} %copy-done.10, bf16[512,2048]{1,0:T(8,128)(2,1)S(1)} %copy-done, bf16[1024,2048]{1,0:T(8,128)(2,1)S(1)} %copy-done.3, bf16[1024,2048]{1,0:T(8,128)(2,1)S(1)} %copy-done.2, f32[1024]{0:T(1024)S(1)} %broadcast_multiply_fusion, ...), kind=kOutput, calls=%fused_computation.36 | convolution fusion | flops 2173173760 | bytes 16797696 | tf_op jit(solution)/shard_map/dot_general | solution.py:118
  247.2 6.7 %convolution_bitcast_fusion = f32[2048,1024]{0,1:T(8,128)} fusion(bf16[1024,1024]{0,1:T(8,128)(2,1)S(1)} %bitcast.75, bf16[1024,2048]{1,0:T(8,128)(2,1)S(1)} %copy-done.2), kind=kOutput, calls=%fused_computation.9 | convolution fusion | flops 4294967296 | bytes 14680064 | tf_op jit(solution)/shard_map/dot_general | solution.py:75
  253.9 11.7 %reshape_reshape_reshape.3 = f32[4,2,256,2,512]{2,1,0,4,3:T(2,128)} reshape(f32[2048,1024]{0,1:T(8,128)} %convolution_bitcast_fusion) | data formatting | bytes 16777216 | tf_op jit(solution)/shard_map/reshape;reshape;reshape | solution.py:19
  265.6 13.1 %copy.24 = f32[2,4,256,2,512]{4,2,3,1,0:T(8,128)} copy(f32[2,4,256,2,512]{2,0,1,4,3:T(2,128)} %bitcast.71) | data formatting | bytes 16777216 | tf_op jit(solution)/shard_map/transpose | solution.py:20
  278.8 19.6 %reduce-scatter.3.cloned.1.call-done = f32[4,256,2,512]{3,1,2,0:T(8,128)} async-done(((f32[8,256,2,512]{3,1,2,0:T(8,128)}), f32[4,256,2,512]{3,1,2,0:T(8,128)}) %reduce-scatter.3.cloned.1.call-update) | async-done | bytes 4194320 | tf_op jit(solution)/shard_map/reduce_scatter | solution.py:23
  299.1 49.6 %reduce-scatter.5.cloned.1.call-done = f32[1,256,2,512]{3,1,2,0:T(8,128)} async-done(((f32[4,256,2,512]{3,1,2,0:T(8,128)}), f32[1,256,2,512]{3,1,2,0:T(8,128)}) %reduce-scatter.5.cloned.1.call-update) | async-done | bytes 1048592 | tf_op jit(solution)/shard_map/reduce_scatter | solution.py:23
  348.7 2.1 multiply_reduce_fusion.1
  350.8 7.1 %all-reduce.3 = (f32[]{:T(128)}, f32[]{:T(128)}) all-reduce(f32[]{:T(128)} %multiply_reduce_fusion.1, f32[]{:T(128)S(6)} %div.55), channel_id=1, replica_groups=mesh['dp_0'=4,'dp_1'=2,'mp_0'=4,'mp_1'=4] {'dp_0'}, use_global_device_ids=true, to_apply=%region_9.10 | all-reduce | flops 2 | bytes 16 | tf_op jit(solution)/shard_map/psum | solution.py:38
  357.9 5.5 %all-reduce.4 = (f32[]{:T(128)}, f32[]{:T(128)}) all-reduce(f32[]{:T(128)} %get-tuple-element.14, f32[]{:T(128)} %get-tuple-element.15), channel_id=1, replica_groups=mesh['dp_0'=4,'dp_1'=2,'mp_0'=4,'mp_1'=4] {'dp_1'}, use_global_device_ids=true, to_apply=%region_10.11 | all-reduce | flops 2 | bytes 16 | tf_op jit(solution)/shard_map/psum | solution.py:38
  363.4 9.0 %all-reduce.2 = (f32[]{:T(128)}, f32[]{:T(128)}) all-reduce(f32[]{:T(128)} %get-tuple-element.16, f32[]{:T(128)} %get-tuple-element.17), channel_id=1, replica_groups=mesh['dp_0'=4,'dp_1'=2,'mp_0'=4,'mp_1'=4] {'mp_0'}, use_global_device_ids=true, to_apply=%region_11.12 | all-reduce | flops 2 | bytes 16 | tf_op jit(solution)/shard_map/psum | solution.py:38
  372.4 9.1 %all-reduce.1 = (f32[]{:T(128)}, f32[]{:T(128)}) all-reduce(f32[]{:T(128)} %get-tuple-element.12, f32[]{:T(128)} %get-tuple-element.13), channel_id=1, replica_groups=mesh['dp_0'=4,'dp_1'=2,'mp_0'=4,'mp_1'=4] {'mp_1'}, use_global_device_ids=true, to_apply=%region_12.13 | all-reduce | flops 2 | bytes 16 | tf_op jit(solution)/shard_map/psum | solution.py:38
  382.2 3.2 fusion.31
  392.2 26.3 %all-gather.2.cloned.1.call-done = bf16[2048,2,512]{2,1,0:T(2,128)(2,1)} async-done(((bf16[256,2,512]{2,1,0:T(2,128)(2,1)}), bf16[2048,2,512]{2,1,0:T(2,128)(2,1)}) %all-gather.2.cloned.1.call-update) | async-done | bytes 4194320 | tf_op jit(solution)/shard_map/all_gather | solution.py:144
  418.4 7.8 %copy.54 = bf16[2048,2,512]{2,1,0:T(2,128)(2,1)} copy(bf16[2048,2,512]{2,1,0:T(2,128)(2,1)} %all-gather.2.cloned.1.call-done) | data formatting | bytes 8388608
  (57 shorter events, 12.0 us)
Async XLA Ops:
  7.2 21.7 %copy-start = (bf16[512,2048]{1,0:T(8,128)(2,1)S(1)}, bf16[512,2048]{1,0:T(8,128)(2,1)}, u32[]{:S(2)}) copy-start(bf16[512,2048]{1,0:T(8,128)(2,1)} %param.17) | copy-start | bytes 6291460
  7.2 122.1 %all-reduce.8.cloned.1.call-start = ((), (), s32[]{:S(2)}) async-start(), calls=%async_computation.2 | async-start | bytes 8388608 | tf_op jit(solution)/shard_map/psum | solution.py:110
  26.9 2.0 copy-start.9
  33.3 96.2 %copy-start.8 = (s32[4]{0:T(128)S(1)}, s32[4]{0:T(128)}, u32[]{:S(2)}) copy-start(s32[4]{0:T(128)} %param.15) | copy-start | bytes 52
  33.3 96.3 %copy-start.5 = (f32[4,256]{1,0:T(4,128)S(1)}, f32[4,256]{1,0:T(4,128)}, u32[]{:S(2)}) copy-start(f32[4,256]{1,0:T(4,128)} %param.13) | copy-start | bytes 12292
  33.3 96.4 %copy-start.4 = (s32[4,256]{1,0:T(4,128)S(1)}, s32[4,256]{1,0:T(4,128)}, u32[]{:S(2)}) copy-start(s32[4,256]{1,0:T(4,128)} %param.14) | copy-start | bytes 12292
  33.3 98.1 %copy-start.7 = (f32[4,256]{1,0:T(4,128)S(1)}, f32[4,256]{1,0:T(4,128)}, u32[]{:S(2)}) copy-start(f32[4,256]{1,0:T(4,128)} %param.12) | copy-start | bytes 12292
  33.4 190.9 %all-reduce.10.cloned.1.call-start = ((), (), s32[]{:S(2)}) async-start(), calls=%async_computation.3 | async-start | bytes 8388608 | tf_op jit(solution)/shard_map/psum | solution.py:109
  129.3 169.1 %reduce-scatter.3.cloned.1.call-start = ((), (), s32[]{:S(2)}) async-start(), calls=%async_computation.4 | async-start | bytes 12582912 | tf_op jit(solution)/shard_map/reduce_scatter | solution.py:23
  132.7 96.6 %copy-start.6 = (f32[2048]{0:T(1024)S(1)}, f32[2048]{0:T(1024)}, u32[]{:S(2)}) copy-start(f32[2048]{0:T(1024)} %param.18) | copy-start | bytes 24580
  224.3 5.1 %copy-start.2 = (bf16[1024,2048]{1,0:T(8,128)(2,1)S(1)}, bf16[1024,2048]{1,0:T(8,128)(2,1)}, u32[]{:S(2)}) copy-start(bf16[1024,2048]{1,0:T(8,128)(2,1)} %param.11) | copy-start | bytes 12582916
  224.3 5.9 %copy-start.3 = (bf16[1024,2048]{1,0:T(8,128)(2,1)S(1)}, bf16[1024,2048]{1,0:T(8,128)(2,1)}, u32[]{:S(2)}) copy-start(bf16[1024,2048]{1,0:T(8,128)(2,1)} %all-reduce.10.cloned.1.call-done) | copy-start | bytes 12582916
  238.9 2.6 copy-start.10
  278.7 70.0 %reduce-scatter.5.cloned.1.call-start = ((), (), s32[]{:S(2)}) async-start(), calls=%async_computation.5 | async-start | bytes 5242880 | tf_op jit(solution)/shard_map/reduce_scatter | solution.py:23
  298.4 120.0 %all-gather.2.cloned.1.call-start = ((), (), s32[]{:S(2)}) async-start(), calls=%async_computation.6 | async-start | bytes 4718592 | tf_op jit(solution)/shard_map/all_gather | solution.py:144
  418.4 7.9 %copy-start.1 = (bf16[512,2048]{1,0:T(8,128)(2,1)S(1)}, bf16[512,2048]{1,0:T(8,128)(2,1)}, u32[]{:S(2)}) copy-start(bf16[512,2048]{1,0:T(8,128)(2,1)} %param.17) | copy-start | bytes 6291460
Sparse Core Ops, SparseCore 0:
  33.5 95.7 all-reduce.7
  131.7 92.5 all-reduce.9
  278.8 19.5 reduce-scatter.2
  300.7 48.0 reduce-scatter.4
  386.9 31.4 all-gather.1
